TPU v7x, 32 devices: a whole 2x2x4 slice. The times are simulated.
32 devices in a mesh: fsdp: 16 (over z, y, core), tp: 2 (over x).
Axes of the slice: x: 2, y: 2, z: 4, core: 2. Of those that a mesh axis runs over, the one named last changes fastest.
Arguments:
- hidden: bfloat16 [32, 5120], P(None, 'fsdp'), may hold values from -20 to 20
- query_weight: bfloat16 [5120, 5120], P(None, ('tp', 'fsdp')), may hold values from -0.078125 to 0.078125
- key_weight: bfloat16 [5120, 1024], P(None, ('tp', 'fsdp')), may hold values from -0.078125 to 0.078125
- value_weight: bfloat16 [5120, 1024], P(None, ('tp', 'fsdp')), may hold values from -0.078125 to 0.078125
- output_weight: bfloat16 [5120, 5120], P(('tp', 'fsdp')), may hold values from -0.078125 to 0.078125
- gate_weight: bfloat16 [5120, 27648], P(None, ('tp', 'fsdp')), may hold values from -0.078125 to 0.078125
- up_weight: bfloat16 [5120, 27648], P(None, ('tp', 'fsdp')), may hold values from -0.078125 to 0.078125
- down_weight: bfloat16 [27648, 5120], P(('tp', 'fsdp')), may hold values from -0.0390625 to 0.0390625
- history: float32 [7, 1024], replicated, may hold values from 0.0001 to 1, as said below
- slot: int32 [1], replicated, may hold values from 0 to 1023
- lengths: int32 [32], P('fsdp'), may hold values from 512 to 4096, as said below
- key_cache: bfloat16 [32, 4096, 1024], P('fsdp', None, 'tp'), may hold values from -1000 to 1000
- value_cache: bfloat16 [32, 4096, 1024], P('fsdp', None, 'tp'), may hold values from -6 to 6
Outputs:
- attention_out: bfloat16 [32, 5120], P('fsdp', 'tp')
- query_rollout: bfloat16 [5120, 5120], P('fsdp', 'tp')
- key_rollout: bfloat16 [5120, 1024], P('fsdp', 'tp')
- value_rollout: bfloat16 [5120, 1024], P('fsdp', 'tp')
- output_rollout: bfloat16 [5120, 5120], P('tp', 'fsdp')
- gate_rollout: bfloat16 [5120, 27648], P('fsdp', 'tp')
- up_rollout: bfloat16 [5120, 27648], P('fsdp', 'tp')
- down_rollout: bfloat16 [27648, 5120], P('tp', 'fsdp')
- new_history: float32 [7, 1024], replicated
Inputs may be any that keep to these rules, and one draw needn't show every extreme that they name: `history`: strictly positive. `lengths`: some sequence has all 4096 slots valid.
All inputs are finite; a program needn't handle non-finite values.
Results may differ from a plain program's by a relative error of at most 0.012.
The roundings to bfloat16 on the way count: a program that leaves them out, or rounds other values in their place, can miss the bound.
Values may be sent and summed in bfloat16 or wider, within the bound.
A program may use at most 192 MiB of HBM per device.

v0:
```python
import jax
import jax.numpy as jnp
from jax import lax
from jax.sharding import PartitionSpec as P

D = 5120
HEADS = 40
KV_HEADS = 8
HEAD_DIM = 128
target_peak = 4.0
norm_eps = 1e-06
rope_theta = 1000000.0


def largest(tensor):
    return jnp.max(jnp.abs(tensor.astype(jnp.float32)))


def scaling(peaks, history, slot):
    marked = lax.broadcasted_iota(jnp.int32, history.shape, 1) == slot[0]
    kept = jnp.max(jnp.where(marked, jnp.zeros_like(history), history), axis=1)
    return (target_peak / jnp.maximum(peaks, kept), jnp.where(marked, peaks[:, None], history))


def quantize(tensor, factor):
    return (tensor.astype(jnp.float32) * factor).astype(jnp.bfloat16)


def rotate(vectors, positions):
    half_dim = vectors.shape[-1] // 2
    ladder = jnp.arange(half_dim, dtype=jnp.float32)
    spread = rope_theta ** (-2.0 * ladder / vectors.shape[-1])
    angle = positions.astype(jnp.float32)[:, None] * spread[None, :]
    cosine = jnp.cos(angle)[:, None, :]
    sine = jnp.sin(angle)[:, None, :]
    first = vectors[..., :half_dim]
    second = vectors[..., half_dim:]
    return jnp.concatenate(
        [first * cosine - second * sine, second * cosine + first * sine], axis=-1
    )


def regroup(query_part, key_part, value_part, output_part, gate_part, up_part, down_part):
    columns = (
        lax.all_to_all(query_part, "fsdp", split_axis=0, concat_axis=1, tiled=True),
        lax.all_to_all(key_part, "fsdp", split_axis=0, concat_axis=1, tiled=True),
        lax.all_to_all(value_part, "fsdp", split_axis=0, concat_axis=1, tiled=True),
        lax.all_to_all(gate_part, "fsdp", split_axis=0, concat_axis=1, tiled=True),
        lax.all_to_all(up_part, "fsdp", split_axis=0, concat_axis=1, tiled=True),
    )
    rowwise = (
        lax.all_to_all(output_part, "fsdp", split_axis=1, concat_axis=0, tiled=True),
        lax.all_to_all(down_part, "fsdp", split_axis=1, concat_axis=0, tiled=True),
    )
    return (columns[0], columns[1], columns[2], rowwise[0], columns[3], columns[4], rowwise[1])


def attend(query, key_new, value_new, key_cache, value_cache, lengths):
    count_seq = query.shape[0]
    kv_count = query.shape[1]
    head_dim = query.shape[3]
    cache_len = key_cache.shape[1]
    keys = key_cache.reshape(count_seq, cache_len, kv_count, head_dim)
    values = value_cache.reshape(count_seq, cache_len, kv_count, head_dim)
    scale = head_dim ** (-0.5)
    scores = jnp.einsum("bkgd,bjkd->bkgj", query, keys, preferred_element_type=jnp.float32) * scale
    own = (
        jnp.sum(query.astype(jnp.float32) * key_new.astype(jnp.float32)[:, :, None, :], axis=-1)
        * scale
    )
    valid = (lax.broadcasted_iota(jnp.int32, (count_seq, cache_len), 1) < lengths[:, None])[
        :, None, None, :
    ]
    top = jnp.maximum(jnp.max(jnp.where(valid, scores, -1e30), axis=-1), own)
    weights = jnp.where(valid, jnp.exp(scores - top[..., None]), 0.0)
    own_weight = jnp.exp(own - top)
    total = jnp.sum(weights, axis=-1) + own_weight
    probs = (weights / total[..., None]).astype(jnp.bfloat16)
    own_prob = (own_weight / total).astype(jnp.bfloat16)
    mixed = jnp.einsum("bkgj,bjkd->bkgd", probs, values, preferred_element_type=jnp.float32)
    mixed = (
        mixed
        + own_prob.astype(jnp.float32)[..., None] * value_new.astype(jnp.float32)[:, :, None, :]
    )
    return mixed.astype(jnp.bfloat16).reshape(count_seq, -1)


def per_device(
    hidden,
    query_weight,
    key_weight,
    value_weight,
    output_weight,
    gate_weight,
    up_weight,
    down_weight,
    history,
    slot,
    lengths,
    key_cache,
    value_cache,
):
    trainer = (
        query_weight,
        key_weight,
        value_weight,
        output_weight,
        gate_weight,
        up_weight,
        down_weight,
    )
    peaks = jnp.stack([lax.pmax(largest(tensor), ("fsdp", "tp")) for tensor in trainer])
    factors, new_history = scaling(peaks, history, slot)
    arrived = regroup(
        query_weight, key_weight, value_weight, output_weight, gate_weight, up_weight, down_weight
    )
    rollout = tuple((quantize(arrived[number], factors[number]) for number in range(7)))
    (
        query_rollout,
        key_rollout,
        value_rollout,
        output_rollout,
        gate_rollout,
        up_rollout,
        down_rollout,
    ) = rollout
    widened = hidden.astype(jnp.float32)
    squares = jnp.sum(widened * widened, axis=1)
    joined = jnp.concatenate([query_rollout, key_rollout, value_rollout], axis=1)
    partial_value = jnp.dot(hidden, joined, preferred_element_type=jnp.float32)
    summed, total_sq = (
        lax.psum_scatter(partial_value, "fsdp", scatter_dimension=0, tiled=True),
        lax.psum_scatter(squares, "fsdp", scatter_dimension=0, tiled=True),
    )
    inv_rms = lax.rsqrt(total_sq / D + norm_eps)[:, None]
    width_q = query_rollout.shape[1]
    width_k = key_rollout.shape[1]
    query = summed[:, :width_q] * inv_rms / factors[0]
    key_new = summed[:, width_q : width_q + width_k] * inv_rms / factors[1]
    value_new = summed[:, width_q + width_k :] * inv_rms / factors[2]
    count_seq = summed.shape[0]
    query = rotate(query.reshape(count_seq, -1, HEAD_DIM), lengths).astype(jnp.bfloat16)
    query = query.reshape(count_seq, -1, HEADS // KV_HEADS, HEAD_DIM)
    key_new = rotate(key_new.reshape(count_seq, -1, HEAD_DIM), lengths).astype(jnp.bfloat16)
    value_new = value_new.reshape(count_seq, -1, HEAD_DIM).astype(jnp.bfloat16)
    attention_out = attend(query, key_new, value_new, key_cache, value_cache, lengths)
    return (
        attention_out,
        query_rollout,
        key_rollout,
        value_rollout,
        output_rollout,
        gate_rollout,
        up_rollout,
        down_rollout,
        new_history,
    )


def solution(mesh):
    return jax.shard_map(
        per_device,
        mesh=mesh,
        in_specs=(
            P(None, "fsdp"),
            P(None, ("tp", "fsdp")),
            P(None, ("tp", "fsdp")),
            P(None, ("tp", "fsdp")),
            P(("tp", "fsdp"), None),
            P(None, ("tp", "fsdp")),
            P(None, ("tp", "fsdp")),
            P(("tp", "fsdp"), None),
            P(),
            P(),
            P("fsdp"),
            P("fsdp", None, "tp"),
            P("fsdp", None, "tp"),
        ),
        out_specs=(
            P("fsdp", "tp"),
            P("fsdp", "tp"),
            P("fsdp", "tp"),
            P("fsdp", "tp"),
            P("tp", "fsdp"),
            P("fsdp", "tp"),
            P("fsdp", "tp"),
            P("tp", "fsdp"),
            P(),
        ),
        check_vma=False,
    )
```

profile of v0, /device:TPU:0, one launch (start us, length us, event | category | flops | bytes accessed | tf_op | source)
XLA Modules:
  0.0 1055.7 jit_solution(7451371705270785353)
XLA Ops:
  7.2 1.3 all_to_all.72
  9.3 7.4 all-to-all-start.1
  18.9 10.0 all-to-all-done.1
  29.6 3.6 all-to-all-start.2
  33.2 3.3 all_to_all.70
  36.5 1.7 copy.68
  38.2 7.1 all-to-all-done.2
  45.3 4.4 all-to-all-start
  49.8 3.3 all_to_all.76
  53.1 1.7 copy.77
  54.8 33.7 %all-to-all-done = bf16[16,320,160]{1,2,0:T(8,128)(2,1)} async-done(((bf16[16,320,160]{1,2,0:T(8,128)(2,1)}), bf16[16,320,160]{1,2,0:T(8,128)(2,1)}, u32[]{:S(2)}, u32[]{:S(2)}) %all-to-all-start) | async-done | bytes 1638432 | tf_op jit(solution)/shard_map/all_to_all | solution.py:45
  88.4 10.7 %all-to-all-start.3 = ((bf16[160,16,320]{2,0,1:T(8,128)(2,1)}), bf16[160,16,320]{2,0,1:T(8,128)(2,1)S(1)}, u32[]{:S(2)}, u32[]{:S(2)}) async-start(bf16[160,16,320]{2,0,1:T(8,128)(2,1)} %copy.77), calls=%async_computation.3 | async-start | bytes 3932160 | tf_op jit(solution)/shard_map/all_to_all | solution.py:52
  99.1 12.7 %copy.78 = bf16[5120,864]{1,0:T(8,128)(2,1)} copy(bf16[5120,864]{0,1:T(8,128)(2,1)} %param.18) | data formatting | bytes 17694720 | tf_op args[5]
  111.8 26.0 %all-to-all-done.3 = bf16[160,16,320]{2,0,1:T(8,128)(2,1)S(1)} async-done(((bf16[160,16,320]{2,0,1:T(8,128)(2,1)}), bf16[160,16,320]{2,0,1:T(8,128)(2,1)S(1)}, u32[]{:S(2)}, u32[]{:S(2)}) %all-to-all-start.3) | async-done | bytes 1638432 | tf_op jit(solution)/shard_map/all_to_all | solution.py:52
  139.1 10.7 %all-to-all-start.4 = ((bf16[16,320,864]{2,1,0:T(8,128)(2,1)}), bf16[16,320,864]{2,1,0:T(8,128)(2,1)}, u32[]{:S(2)}, u32[]{:S(2)}) async-start(bf16[16,320,864]{2,1,0:T(8,128)(2,1)} %bitcast.74), calls=%async_computation.4 | async-start | bytes 18350080 | tf_op jit(solution)/shard_map/all_to_all | solution.py:48
  149.8 12.7 %copy.80 = bf16[5120,864]{1,0:T(8,128)(2,1)} copy(bf16[5120,864]{0,1:T(8,128)(2,1)} %param.19) | data formatting | bytes 17694720 | tf_op args[6]
  162.5 151.6 %all-to-all-done.4 = bf16[16,320,864]{2,1,0:T(8,128)(2,1)} async-done(((bf16[16,320,864]{2,1,0:T(8,128)(2,1)}), bf16[16,320,864]{2,1,0:T(8,128)(2,1)}, u32[]{:S(2)}, u32[]{:S(2)}) %all-to-all-start.4) | async-done | bytes 8847392 | tf_op jit(solution)/shard_map/all_to_all | solution.py:48
  314.1 39.7 %all-to-all-start.5 = ((bf16[16,320,864]{2,1,0:T(8,128)(2,1)}), bf16[16,320,864]{2,1,0:T(8,128)(2,1)}, u32[]{:S(2)}, u32[]{:S(2)}) async-start(bf16[16,320,864]{2,1,0:T(8,128)(2,1)} %bitcast.75), calls=%async_computation.5 | async-start | bytes 18350080 | tf_op jit(solution)/shard_map/all_to_all | solution.py:49
  353.8 12.7 %copy.82 = bf16[864,5120]{0,1:T(8,128)(2,1)} copy(bf16[864,5120]{1,0:T(8,128)(2,1)} %param.20) | data formatting | bytes 17694720 | tf_op args[7]
  366.5 151.6 %all-to-all-done.5 = bf16[16,320,864]{2,1,0:T(8,128)(2,1)} async-done(((bf16[16,320,864]{2,1,0:T(8,128)(2,1)}), bf16[16,320,864]{2,1,0:T(8,128)(2,1)}, u32[]{:S(2)}, u32[]{:S(2)}) %all-to-all-start.5) | async-done | bytes 8847392 | tf_op jit(solution)/shard_map/all_to_all | solution.py:49
  518.1 40.0 %all-to-all-start.6 = ((bf16[864,16,320]{0,2,1:T(8,128)(2,1)}), bf16[864,16,320]{0,2,1:T(8,128)(2,1)}, u32[]{:S(2)}, u32[]{:S(2)}) async-start(bf16[864,16,320]{0,2,1:T(8,128)(2,1)} %bitcast.73), calls=%async_computation.6 | async-start | bytes 18350080 | tf_op jit(solution)/shard_map/all_to_all | solution.py:53
  558.4 1.6 abs_reduce_fusion.6
  560.0 1.6 abs_reduce_fusion.5
  563.3 5.9 abs_reduce_fusion.2
  569.3 5.8 abs_reduce_fusion.1
  575.1 2.3 abs_reduce_fusion
  577.4 201.6 %all-reduce.2 = (f32[1]{0:T(128)}, f32[1]{0:T(128)}, f32[1]{0:T(128)}, f32[1]{0:T(128)}, f32[1]{0:T(128)}, /*index=5*/f32[1]{0:T(128)}, f32[1]{0:T(128)}) all-reduce(f32[1]{0:T(128)} %bitcast, f32[1]{0:T(128)} %bitcast.1, f32[1]{0:T(128)} %bitcast.2, f32[1]{0:T(128)} %bitcast.3, ...), channel_id=1, replica_groups=mesh['fsdp'=16,'tp'=2] {'fsdp','tp'}, use_global_device_ids=true, to_apply=%region_1.0 | all-reduce | flops 7 | bytes 56 | tf_op jit(solution)/shard_map/pmax | solution.py:112
  781.0 4.5 stack.31
  785.7 31.4 %all-reduce.1 = f32[32]{0:T(128)S(1)} all-reduce(f32[32]{0:T(128)S(1)} %multiply_reduce_fusion), channel_id=3, replica_groups=mesh['fsdp'=16,'tp'=2] {'fsdp'}, use_global_device_ids=true, to_apply=%region_17.18.clone | all-reduce | flops 32 | bytes 256
  822.0 2.6 multiply_convert_fusion.4
  824.6 3.3 copy.84
  827.8 1.7 convolution_bitcast_fusion
  829.6 2.6 multiply_convert_fusion.3
  832.1 3.8 copy.87
  835.9 81.5 %all-reduce.5.cloned.1.call-done = f32[32,3584]{1,0:T(8,128)} async-done(((f32[32,3584]{1,0:T(8,128)}), f32[32,3584]{1,0:T(8,128)}) %all-reduce.5.cloned.1.call-update) | async-done | bytes 458768
  917.4 2.1 fusion.32
  919.5 1.6 fusion.28
  921.6 5.8 select_reduce_fusion
  927.9 4.7 fusion.20
  933.3 9.7 fusion
  943.0 12.4 %copy.79 = bf16[320,16,864]{2,1,0:T(8,128)(2,1)} copy(bf16[320,16,864]{2,0,1:T(8,128)(2,1)} %fusion) | data formatting | bytes 17694720 | tf_op jit(solution)/shard_map/convert_element_type | solution.py:26
  955.4 16.3 %convert_element_type.218 = bf16[320,13824]{1,0:T(8,128)(2,1)} reshape(bf16[320,16,864]{2,1,0:T(8,128)(2,1)} %copy.79) | data formatting | bytes 17694720 | tf_op jit(solution)/shard_map/convert_element_type | solution.py:26
  971.7 9.8 fusion.1
  981.5 12.4 %copy.81 = bf16[320,16,864]{2,1,0:T(8,128)(2,1)} copy(bf16[320,16,864]{2,0,1:T(8,128)(2,1)} %fusion.1) | data formatting | bytes 17694720 | tf_op jit(solution)/shard_map/convert_element_type | solution.py:26
  993.9 16.3 %convert_element_type.222 = bf16[320,13824]{1,0:T(8,128)(2,1)} reshape(bf16[320,16,864]{2,1,0:T(8,128)(2,1)} %copy.81) | data formatting | bytes 17694720 | tf_op jit(solution)/shard_map/convert_element_type | solution.py:26
  1010.3 9.8 fusion.2
  1020.1 12.4 %copy.83 = bf16[16,864,320]{1,0,2:T(8,128)(2,1)} copy(bf16[16,864,320]{1,2,0:T(8,128)(2,1)} %fusion.2) | data formatting | bytes 17694720 | tf_op jit(solution)/shard_map/convert_element_type | solution.py:26
  1032.4 16.1 %convert_element_type.226 = bf16[13824,320]{0,1:T(8,128)(2,1)} reshape(bf16[16,864,320]{1,0,2:T(8,128)(2,1)} %copy.83) | data formatting | bytes 17694720 | tf_op jit(solution)/shard_map/convert_element_type | solution.py:26
  (67 shorter events, 14.3 us)
Async XLA Ops:
  9.3 19.6 %all-to-all-start.1 = ((bf16[16,320,32]{1,2,0:T(8,128)(2,1)}), bf16[16,320,32]{1,2,0:T(8,128)(2,1)S(1)}, u32[]{:S(2)}, u32[]{:S(2)}) async-start(bf16[16,320,32]{1,2,0:T(8,128)(2,1)} %copy.69), calls=%async_computation.1 | async-start | bytes 786432 | tf_op jit(solution)/shard_map/all_to_all | solution.py:46
  28.9 0.7 copy-start.3
  29.6 15.7 %all-to-all-start.2 = ((bf16[16,320,32]{1,2,0:T(8,128)(2,1)}), bf16[16,320,32]{1,2,0:T(8,128)(2,1)S(1)}, u32[]{:S(2)}, u32[]{:S(2)}) async-start(bf16[16,320,32]{1,2,0:T(8,128)(2,1)} %copy.70), calls=%async_computation.2 | async-start | bytes 786432 | tf_op jit(solution)/shard_map/all_to_all | solution.py:47
  45.3 66.5 %copy-start.5 = (bf16[16,320,32]{1,2,0:T(8,128)(2,1)}, bf16[16,320,32]{1,2,0:T(8,128)(2,1)S(1)}, u32[]{:S(2)}) copy-start(bf16[16,320,32]{1,2,0:T(8,128)(2,1)S(1)} %all-to-all-done.2) | copy-start | bytes 983044
  45.3 43.1 %all-to-all-start = ((bf16[16,320,160]{1,2,0:T(8,128)(2,1)}), bf16[16,320,160]{1,2,0:T(8,128)(2,1)}, u32[]{:S(2)}, u32[]{:S(2)}) async-start(bf16[16,320,160]{1,2,0:T(8,128)(2,1)} %copy.68), calls=%async_computation | async-start | bytes 3932160 | tf_op jit(solution)/shard_map/all_to_all | solution.py:45
  88.4 49.4 %all-to-all-start.3 = ((bf16[160,16,320]{2,0,1:T(8,128)(2,1)}), bf16[160,16,320]{2,0,1:T(8,128)(2,1)S(1)}, u32[]{:S(2)}, u32[]{:S(2)}) async-start(bf16[160,16,320]{2,0,1:T(8,128)(2,1)} %copy.77), calls=%async_computation.3 | async-start | bytes 3932160 | tf_op jit(solution)/shard_map/all_to_all | solution.py:52
  137.8 1.3 copy-start
  139.1 175.0 %all-to-all-start.4 = ((bf16[16,320,864]{2,1,0:T(8,128)(2,1)}), bf16[16,320,864]{2,1,0:T(8,128)(2,1)}, u32[]{:S(2)}, u32[]{:S(2)}) async-start(bf16[16,320,864]{2,1,0:T(8,128)(2,1)} %bitcast.74), calls=%async_computation.4 | async-start | bytes 18350080 | tf_op jit(solution)/shard_map/all_to_all | solution.py:48
  314.1 204.0 %all-to-all-start.5 = ((bf16[16,320,864]{2,1,0:T(8,128)(2,1)}), bf16[16,320,864]{2,1,0:T(8,128)(2,1)}, u32[]{:S(2)}, u32[]{:S(2)}) async-start(bf16[16,320,864]{2,1,0:T(8,128)(2,1)} %bitcast.75), calls=%async_computation.5 | async-start | bytes 18350080 | tf_op jit(solution)/shard_map/all_to_all | solution.py:49
  518.1 43.6 %copy-start.1 = (bf16[5120,160]{0,1:T(8,128)(2,1)S(1)}, bf16[5120,160]{0,1:T(8,128)(2,1)}, u32[]{:S(2)}) copy-start(bf16[5120,160]{0,1:T(8,128)(2,1)} %param.14) | copy-start | bytes 4915204
  518.1 44.4 %copy-start.2 = (bf16[160,5120]{1,0:T(8,128)(2,1)S(1)}, bf16[160,5120]{1,0:T(8,128)(2,1)}, u32[]{:S(2)}) copy-start(bf16[160,5120]{1,0:T(8,128)(2,1)} %param.17) | copy-start | bytes 4915204
  518.1 492.2 %all-to-all-start.6 = ((bf16[864,16,320]{0,2,1:T(8,128)(2,1)}), bf16[864,16,320]{0,2,1:T(8,128)(2,1)}, u32[]{:S(2)}, u32[]{:S(2)}) async-start(bf16[864,16,320]{0,2,1:T(8,128)(2,1)} %bitcast.73), calls=%async_computation.6 | async-start | bytes 18350080 | tf_op jit(solution)/shard_map/all_to_all | solution.py:53
  558.1 359.4 %all-reduce.5.cloned.1.call-start = ((), (), s32[]{:S(2)}) async-start(), calls=%async_computation.7 | async-start | bytes 917504
  563.3 11.8 %slice-start = ((s8[8847360]{0:T(1024)(128)(4,1)}), s8[4194304]{0:T(1024)(128)(4,1)S(1)}, s32[]{:S(2)}) async-start(s8[8847360]{0:T(1024)(128)(4,1)} %bitcast.76), calls=%async_computation.8 | async-start | bytes 8388608
  563.3 11.8 %slice-start.1 = ((s8[8847360]{0:T(1024)(128)(4,1)}), s8[4194304]{0:T(1024)(128)(4,1)S(1)}, s32[]{:S(2)}) async-start(s8[8847360]{0:T(1024)(128)(4,1)} %bitcast.76), calls=%async_computation.9 | async-start | bytes 8388608
  569.2 5.9 slice-start.2
  569.2 210.5 %copy-start.9 = (s32[2]{0:T(128)S(1)}, s32[2]{0:T(128)}, u32[]{:S(2)}) copy-start(s32[2]{0:T(128)} %param.23) | copy-start | bytes 28
  569.2 210.5 %copy-start.10 = (u32[32]{0:T(128)S(1)}, u32[32]{0:T(128)}, u32[]{:S(2)}) copy-start(u32[32]{0:T(128)} %constant.29) | copy-start | bytes 388
  569.2 216.3 %copy-start.8 = (bf16[32,320]{1,0:T(8,128)(2,1)S(1)}, bf16[32,320]{1,0:T(8,128)(2,1)}, u32[]{:S(2)}) copy-start(bf16[32,320]{1,0:T(8,128)(2,1)} %param.13) | copy-start | bytes 61444
  569.2 247.9 %copy-start.7 = (f32[7,1024]{1,0:T(8,128)S(1)}, f32[7,1024]{1,0:T(8,128)}, u32[]{:S(2)}) copy-start(f32[7,1024]{1,0:T(8,128)} %param.21) | copy-start | bytes 86020
  569.2 249.6 %copy-start.4 = (bf16[16,320,32]{1,2,0:T(8,128)(2,1)S(1)}, bf16[16,320,32]{1,2,0:T(8,128)(2,1)}, u32[]{:S(2)}) copy-start(bf16[16,320,32]{1,2,0:T(8,128)(2,1)} %copy-done.3) | copy-start | bytes 983044
  569.3 251.2 %copy-start.6 = (bf16[16,320,32]{1,2,0:T(8,128)(2,1)S(1)}, bf16[16,320,32]{1,2,0:T(8,128)(2,1)}, u32[]{:S(2)}) copy-start(bf16[16,320,32]{1,2,0:T(8,128)(2,1)} %copy-done.5) | copy-start | bytes 983044
Sparse Core Ops, SparseCore 0:
  829.7 87.6 all-reduce.4
where the time goes:
time: 1060 us
  waiting for transfers between devices  461 us (43%)
  blocking collectives  233 us (22%)
  local copies, waits for them, and re-layouts  156 us (15%)
  starting transfers between devices  117 us (11%)
  other arithmetic  60.6 us (6%)
  between operations  15.9 us (2%)
  matrix products  12.2 us (1%)
    pmax x1, blocking collectives, per_device(): lax.pmax(largest(tensor), ('fsdp', 'tp'))  202 us
    all_to_all x1, waiting for transfers between devices, regroup(): lax.all_to_all(gate_part, 'fsdp', split_axis=0, concat_axis=1, tiled=True)  152 us
    all_to_all x1, waiting for transfers between devices, regroup(): lax.all_to_all(up_part, 'fsdp', split_axis=0, concat_axis=1, tiled=True)  152 us
    convert_element_type x6, local copies, waits for them, and re-layouts, quantize(): return (tensor.astype(jnp.float32) * factor).astype(jnp.bfloat16)  86 us
    unnamed x2, waiting for transfers between devices  81.5 us
    unnamed x36, local copies, waits for them, and re-layouts  49.6 us
    all_to_all x1, starting transfers between devices, regroup(): lax.all_to_all(down_part, 'fsdp', split_axis=1, concat_axis=0, tiled=True)  40 us
    all_to_all x1, starting transfers between devices, regroup(): lax.all_to_all(up_part, 'fsdp', split_axis=0, concat_axis=1, tiled=True)  39.7 us
  transfers between devices with their start and end apart: 8, of which 7 were waited for; matrix products, arithmetic and copies ran while one was open for 17% of the time, Pallas kernels for 0%

commit v1 on v0

--- a/solution.py
+++ b/solution.py
@@ -10,6 +10,12 @@
 target_peak = 4.0
 norm_eps = 1e-06
 rope_theta = 1000000.0
+
+
+def exchange_blocks(x, axis, split, join):
+    shards = jnp.split(x, lax.axis_size(axis), axis=split)
+    incoming = lax.all_to_all(jnp.stack(shards), axis, 0, 0)
+    return jnp.concatenate(incoming, axis=join)
 
 
 def largest(tensor):
@@ -45,7 +51,7 @@
         lax.all_to_all(query_part, "fsdp", split_axis=0, concat_axis=1, tiled=True),
         lax.all_to_all(key_part, "fsdp", split_axis=0, concat_axis=1, tiled=True),
         lax.all_to_all(value_part, "fsdp", split_axis=0, concat_axis=1, tiled=True),
-        lax.all_to_all(gate_part, "fsdp", split_axis=0, concat_axis=1, tiled=True),
+        exchange_blocks(gate_part, "fsdp", 0, 1),
         lax.all_to_all(up_part, "fsdp", split_axis=0, concat_axis=1, tiled=True),
     )
     rowwise = (

time: 1060 us -> 1070 us (level)
  local copies, waits for them, and re-layouts: 156 us -> 208 us
  waiting for transfers between devices: 461 us -> 416 us
    unnamed x36 -> x74, local copies, waits for them, and re-layouts: 49.6 us -> 92.4 us
    all_to_all x1, waiting for transfers between devices: 26 us -> 0.01 us  [regroup(): lax.all_to_all(output_part, 'fsdp', split_axis=1, concat_axis=0, tiled=True)]
    all_to_all x1, waiting for transfers between devices: 33.7 us -> 13.6 us  [regroup(): lax.all_to_all(query_part, 'fsdp', split_axis=0, concat_axis=1, tiled=True)]
  transfers between devices with their start and end apart: 8 -> 8, of which waited for: 7 -> 6; matrix products, arithmetic and copies ran while one was open for 17% -> 22% of each run, Pallas kernels for 0% -> 0%
where the time goes in v1:
time: 1070 us; the launch traced here: 1060 us
  waiting for transfers between devices  416 us (39%)
  blocking collectives  233 us (22%)
  local copies, waits for them, and re-layouts  208 us (19%)
  starting transfers between devices  112 us (10%)
  other arithmetic  60.3 us (6%)
  between operations  15.8 us (1%)
  matrix products  12.2 us (1%)
    pmax x1, blocking collectives, per_device(): lax.pmax(largest(tensor), ('fsdp', 'tp'))  202 us
    all_to_all x1, waiting for transfers between devices, exchange_blocks(): incoming = lax.all_to_all(jnp.stack(shards), axis, 0, 0)  152 us
    all_to_all x1, waiting for transfers between devices, regroup(): lax.all_to_all(up_part, 'fsdp', split_axis=0, concat_axis=1, tiled=True)  151 us
    unnamed x74, local copies, waits for them, and re-layouts  92.4 us
    convert_element_type x6, local copies, waits for them, and re-layouts, quantize(): return (tensor.astype(jnp.float32) * factor).astype(jnp.bfloat16)  86.2 us
    unnamed x2, waiting for transfers between devices  81.8 us
    all_to_all x1, starting transfers between devices, regroup(): lax.all_to_all(down_part, 'fsdp', split_axis=1, concat_axis=0, tiled=True)  40 us
    all_to_all x1, starting transfers between devices, regroup(): lax.all_to_all(up_part, 'fsdp', split_axis=0, concat_axis=1, tiled=True)  39.9 us
  transfers between devices with their start and end apart: 8, of which 6 were waited for; matrix products, arithmetic and copies ran while one was open for 22% of the time, Pallas kernels for 0%

profile of v1, /device:TPU:0, one launch (start us, length us, event | category | flops | bytes accessed | tf_op | source)
XLA Modules:
  0.0 1056.9 jit_solution(5502298691678608252)
XLA Ops:
  9.3 7.4 all-to-all-start.1
  18.9 10.0 all-to-all-done.1
  29.7 3.6 all-to-all-start.2
  33.2 3.3 all_to_all.63
  38.2 7.1 all-to-all-done.2
  46.1 4.4 all-to-all-start
  50.5 7.8 fusion.40
  58.4 2.2 copy.136
  60.5 2.2 copy.137
  64.9 3.3 all_to_all.69
  75.7 13.6 %all-to-all-done = bf16[16,320,160]{1,2,0:T(8,128)(2,1)} async-done(((bf16[16,320,160]{1,2,0:T(8,128)(2,1)}), bf16[16,320,160]{1,2,0:T(8,128)(2,1)}, u32[]{:S(2)}, u32[]{:S(2)}) %all-to-all-start) | async-done | bytes 1638432 | tf_op jit(solution)/shard_map/all_to_all | solution.py:51
  89.2 10.7 %all-to-all-start.3 = ((bf16[160,16,320]{2,0,1:T(8,128)(2,1)}), bf16[160,16,320]{2,0,1:T(8,128)(2,1)S(1)}, u32[]{:S(2)}, u32[]{:S(2)}) async-start(bf16[160,16,320]{2,0,1:T(8,128)(2,1)} %copy.110), calls=%async_computation.3 | async-start | bytes 3932160 | tf_op jit(solution)/shard_map/all_to_all | solution.py:58
  104.0 2.2 copy.141
  106.2 2.2 copy.142
  108.4 2.2 copy.143
  112.7 2.2 copy.145
  114.8 2.2 copy.146
  119.2 2.2 copy.148
  121.3 2.2 copy.149
  144.8 6.1 all-to-all-start.4
  150.8 12.7 %copy.128 = bf16[5120,864]{1,0:T(8,128)(2,1)} copy(bf16[5120,864]{0,1:T(8,128)(2,1)} %param.19) | data formatting | bytes 17694720 | tf_op args[6]
  163.6 151.5 %all-to-all-done.4 = bf16[16,320,864]{2,1,0:T(8,128)(2,1)} async-done(((bf16[16,320,864]{2,1,0:T(8,128)(2,1)}), bf16[16,320,864]{2,1,0:T(8,128)(2,1)}, u32[]{:S(2)}, u32[]{:S(2)}) %all-to-all-start.4) | async-done | bytes 8847392 | tf_op jit(solution)/shard_map/all_to_all | solution.py:17
  315.1 39.9 %all-to-all-start.5 = ((bf16[16,320,864]{2,1,0:T(8,128)(2,1)}), bf16[16,320,864]{2,1,0:T(8,128)(2,1)}, u32[]{:S(2)}, u32[]{:S(2)}) async-start(bf16[16,320,864]{2,1,0:T(8,128)(2,1)} %bitcast.105), calls=%async_computation.5 | async-start | bytes 18350080 | tf_op jit(solution)/shard_map/all_to_all | solution.py:55
  355.0 12.8 %copy.130 = bf16[864,5120]{0,1:T(8,128)(2,1)} copy(bf16[864,5120]{1,0:T(8,128)(2,1)} %param.20) | data formatting | bytes 17694720 | tf_op args[7]
  367.8 151.5 %all-to-all-done.5 = bf16[16,320,864]{2,1,0:T(8,128)(2,1)} async-done(((bf16[16,320,864]{2,1,0:T(8,128)(2,1)}), bf16[16,320,864]{2,1,0:T(8,128)(2,1)}, u32[]{:S(2)}, u32[]{:S(2)}) %all-to-all-start.5) | async-done | bytes 8847392 | tf_op jit(solution)/shard_map/all_to_all | solution.py:55
  519.3 40.0 %all-to-all-start.6 = ((bf16[864,16,320]{0,2,1:T(8,128)(2,1)}), bf16[864,16,320]{0,2,1:T(8,128)(2,1)}, u32[]{:S(2)}, u32[]{:S(2)}) async-start(bf16[864,16,320]{0,2,1:T(8,128)(2,1)} %bitcast.104), calls=%async_computation.6 | async-start | bytes 18350080 | tf_op jit(solution)/shard_map/all_to_all | solution.py:59
  564.2 5.9 abs_reduce_fusion.2
  570.1 5.9 abs_reduce_fusion.1
  576.0 2.2 abs_reduce_fusion
  578.2 202.0 %all-reduce.2 = (f32[1]{0:T(128)}, f32[1]{0:T(128)}, f32[1]{0:T(128)}, f32[1]{0:T(128)}, f32[1]{0:T(128)}, /*index=5*/f32[1]{0:T(128)}, f32[1]{0:T(128)}) all-reduce(f32[1]{0:T(128)} %bitcast, f32[1]{0:T(128)} %bitcast.1, f32[1]{0:T(128)} %bitcast.2, f32[1]{0:T(128)} %bitcast.3, ...), channel_id=1, replica_groups=mesh['fsdp'=16,'tp'=2] {'fsdp','tp'}, use_global_device_ids=true, to_apply=%region_1.0 | all-reduce | flops 7 | bytes 56 | tf_op jit(solution)/shard_map/pmax | solution.py:118
  782.2 4.6 stack.82
  786.9 31.4 %all-reduce.1 = f32[32]{0:T(128)S(1)} all-reduce(f32[32]{0:T(128)S(1)} %multiply_reduce_fusion), channel_id=3, replica_groups=mesh['fsdp'=16,'tp'=2] {'fsdp'}, use_global_device_ids=true, to_apply=%region_17.18.clone | all-reduce | flops 32 | bytes 256
  823.2 2.5 multiply_convert_fusion.4
  825.7 3.3 copy.132
  830.7 2.6 multiply_convert_fusion.3
  833.3 3.4 copy.135
  836.8 81.8 %all-reduce.5.cloned.1.call-done = f32[32,3584]{1,0:T(8,128)} async-done(((f32[32,3584]{1,0:T(8,128)}), f32[32,3584]{1,0:T(8,128)}) %all-reduce.5.cloned.1.call-update) | async-done | bytes 458768
  922.7 5.8 select_reduce_fusion
  928.9 4.7 fusion.20
  934.3 9.7 fusion
  944.0 12.4 %copy.127 = bf16[320,16,864]{2,1,0:T(8,128)(2,1)} copy(bf16[320,16,864]{2,0,1:T(8,128)(2,1)} %fusion) | data formatting | bytes 17694720 | tf_op jit(solution)/shard_map/convert_element_type | solution.py:32
  956.4 16.5 %convert_element_type.218 = bf16[320,13824]{1,0:T(8,128)(2,1)} reshape(bf16[320,16,864]{2,1,0:T(8,128)(2,1)} %copy.127) | data formatting | bytes 17694720 | tf_op jit(solution)/shard_map/convert_element_type | solution.py:32
  973.0 9.7 fusion.1
  982.7 12.5 %copy.129 = bf16[320,16,864]{2,1,0:T(8,128)(2,1)} copy(bf16[320,16,864]{2,0,1:T(8,128)(2,1)} %fusion.1) | data formatting | bytes 17694720 | tf_op jit(solution)/shard_map/convert_element_type | solution.py:32
  995.2 16.3 %convert_element_type.222 = bf16[320,13824]{1,0:T(8,128)(2,1)} reshape(bf16[320,16,864]{2,1,0:T(8,128)(2,1)} %copy.129) | data formatting | bytes 17694720 | tf_op jit(solution)/shard_map/convert_element_type | solution.py:32
  1011.5 9.9 fusion.2
  1021.3 12.4 %copy.131 = bf16[16,864,320]{1,0,2:T(8,128)(2,1)} copy(bf16[16,864,320]{1,2,0:T(8,128)(2,1)} %fusion.2) | data formatting | bytes 17694720 | tf_op jit(solution)/shard_map/convert_element_type | solution.py:32
  1033.7 16.1 %convert_element_type.226 = bf16[13824,320]{0,1:T(8,128)(2,1)} reshape(bf16[16,864,320]{1,0,2:T(8,128)(2,1)} %copy.131) | data formatting | bytes 17694720 | tf_op jit(solution)/shard_map/convert_element_type | solution.py:32
  (107 shorter events, 64.3 us)
Async XLA Ops:
  9.3 19.6 %all-to-all-start.1 = ((bf16[16,320,32]{1,2,0:T(8,128)(2,1)}), bf16[16,320,32]{1,2,0:T(8,128)(2,1)S(1)}, u32[]{:S(2)}, u32[]{:S(2)}) async-start(bf16[16,320,32]{1,2,0:T(8,128)(2,1)} %copy.102), calls=%async_computation.1 | async-start | bytes 786432 | tf_op jit(solution)/shard_map/all_to_all | solution.py:52
  28.9 0.8 copy-start.7
  29.7 15.7 %all-to-all-start.2 = ((bf16[16,320,32]{1,2,0:T(8,128)(2,1)}), bf16[16,320,32]{1,2,0:T(8,128)(2,1)S(1)}, u32[]{:S(2)}, u32[]{:S(2)}) async-start(bf16[16,320,32]{1,2,0:T(8,128)(2,1)} %copy.103), calls=%async_computation.2 | async-start | bytes 786432 | tf_op jit(solution)/shard_map/all_to_all | solution.py:53
  45.4 0.7 copy-start.9
  46.1 43.1 %all-to-all-start = ((bf16[16,320,160]{1,2,0:T(8,128)(2,1)}), bf16[16,320,160]{1,2,0:T(8,128)(2,1)}, u32[]{:S(2)}, u32[]{:S(2)}) async-start(bf16[16,320,160]{1,2,0:T(8,128)(2,1)} %copy.101), calls=%async_computation | async-start | bytes 3932160 | tf_op jit(solution)/shard_map/all_to_all | solution.py:51
  89.2 55.5 %all-to-all-start.3 = ((bf16[160,16,320]{2,0,1:T(8,128)(2,1)}), bf16[160,16,320]{2,0,1:T(8,128)(2,1)S(1)}, u32[]{:S(2)}, u32[]{:S(2)}) async-start(bf16[160,16,320]{2,0,1:T(8,128)(2,1)} %copy.110), calls=%async_computation.3 | async-start | bytes 3932160 | tf_op jit(solution)/shard_map/all_to_all | solution.py:58
  124.6 18.4 %copy-start.3 = (bf16[320,864]{1,0:T(8,128)(2,1)S(1)}, bf16[320,864]{1,0:T(8,128)(2,1)}, u32[]{:S(2)}) copy-start(bf16[320,864]{1,0:T(8,128)(2,1)} %copy.150) | copy-start | bytes 1658884
  125.7 15.5 %copy-start.6 = (bf16[320,864]{1,0:T(8,128)(2,1)S(1)}, bf16[320,864]{1,0:T(8,128)(2,1)}, u32[]{:S(2)}) copy-start(bf16[320,864]{1,0:T(8,128)(2,1)} %copy.148) | copy-start | bytes 1658884
  125.7 16.4 %copy-start.5 = (bf16[320,864]{1,0:T(8,128)(2,1)S(1)}, bf16[320,864]{1,0:T(8,128)(2,1)}, u32[]{:S(2)}) copy-start(bf16[320,864]{1,0:T(8,128)(2,1)} %copy.149) | copy-start | bytes 1658884
  125.7 18.2 %copy-start.4 = (bf16[320,864]{1,0:T(8,128)(2,1)S(1)}, bf16[320,864]{1,0:T(8,128)(2,1)}, u32[]{:S(2)}) copy-start(bf16[320,864]{1,0:T(8,128)(2,1)} %copy.151) | copy-start | bytes 1658884
  144.8 18.8 %copy-start = (bf16[160,16,320]{2,0,1:T(8,128)(2,1)}, bf16[160,16,320]{2,0,1:T(8,128)(2,1)S(1)}, u32[]{:S(2)}) copy-start(bf16[160,16,320]{2,0,1:T(8,128)(2,1)S(1)} %all-to-all-done.3) | copy-start | bytes 4915204
  144.8 170.3 %all-to-all-start.4 = ((bf16[16,320,864]{2,1,0:T(8,128)(2,1)}), bf16[16,320,864]{2,1,0:T(8,128)(2,1)}, u32[]{:S(2)}, u32[]{:S(2)}) async-start(bf16[16,320,864]{2,1,0:T(8,128)(2,1)} %bitcast_dynamic-update-slice_fusion), calls=%async_computation.4 | async-start | bytes 18350080 | tf_op jit(solution)/shard_map/all_to_all | solution.py:17
  315.1 204.2 %all-to-all-start.5 = ((bf16[16,320,864]{2,1,0:T(8,128)(2,1)}), bf16[16,320,864]{2,1,0:T(8,128)(2,1)}, u32[]{:S(2)}, u32[]{:S(2)}) async-start(bf16[16,320,864]{2,1,0:T(8,128)(2,1)} %bitcast.105), calls=%async_computation.5 | async-start | bytes 18350080 | tf_op jit(solution)/shard_map/all_to_all | solution.py:55
  519.3 43.3 %copy-start.1 = (bf16[5120,160]{0,1:T(8,128)(2,1)S(1)}, bf16[5120,160]{0,1:T(8,128)(2,1)}, u32[]{:S(2)}) copy-start(bf16[5120,160]{0,1:T(8,128)(2,1)} %param.14) | copy-start | bytes 4915204
  519.3 44.1 %copy-start.2 = (bf16[160,5120]{1,0:T(8,128)(2,1)S(1)}, bf16[160,5120]{1,0:T(8,128)(2,1)}, u32[]{:S(2)}) copy-start(bf16[160,5120]{1,0:T(8,128)(2,1)} %param.17) | copy-start | bytes 4915204
  519.3 492.2 %all-to-all-start.6 = ((bf16[864,16,320]{0,2,1:T(8,128)(2,1)}), bf16[864,16,320]{0,2,1:T(8,128)(2,1)}, u32[]{:S(2)}, u32[]{:S(2)}) async-start(bf16[864,16,320]{0,2,1:T(8,128)(2,1)} %bitcast.104), calls=%async_computation.6 | async-start | bytes 18350080 | tf_op jit(solution)/shard_map/all_to_all | solution.py:59
  559.2 359.4 %all-reduce.5.cloned.1.call-start = ((), (), s32[]{:S(2)}) async-start(), calls=%async_computation.7 | async-start | bytes 917504
  564.1 11.8 %slice-start = ((s8[8847360]{0:T(1024)(128)(4,1)}), s8[4194304]{0:T(1024)(128)(4,1)S(1)}, s32[]{:S(2)}) async-start(s8[8847360]{0:T(1024)(128)(4,1)} %bitcast.106), calls=%async_computation.8 | async-start | bytes 8388608
  564.1 11.8 %slice-start.1 = ((s8[8847360]{0:T(1024)(128)(4,1)}), s8[4194304]{0:T(1024)(128)(4,1)S(1)}, s32[]{:S(2)}) async-start(s8[8847360]{0:T(1024)(128)(4,1)} %bitcast.106), calls=%async_computation.9 | async-start | bytes 8388608
  570.1 5.9 slice-start.2
  570.1 210.8 %copy-start.13 = (s32[2]{0:T(128)S(1)}, s32[2]{0:T(128)}, u32[]{:S(2)}) copy-start(s32[2]{0:T(128)} %param.23) | copy-start | bytes 28
  570.1 210.8 %copy-start.14 = (u32[32]{0:T(128)S(1)}, u32[32]{0:T(128)}, u32[]{:S(2)}) copy-start(u32[32]{0:T(128)} %constant.29) | copy-start | bytes 388
  570.1 216.7 %copy-start.12 = (bf16[32,320]{1,0:T(8,128)(2,1)S(1)}, bf16[32,320]{1,0:T(8,128)(2,1)}, u32[]{:S(2)}) copy-start(bf16[32,320]{1,0:T(8,128)(2,1)} %param.13) | copy-start | bytes 61444
  570.1 248.3 %copy-start.11 = (f32[7,1024]{1,0:T(8,128)S(1)}, f32[7,1024]{1,0:T(8,128)}, u32[]{:S(2)}) copy-start(f32[7,1024]{1,0:T(8,128)} %param.21) | copy-start | bytes 86020
  570.1 250.0 %copy-start.8 = (bf16[16,320,32]{1,2,0:T(8,128)(2,1)S(1)}, bf16[16,320,32]{1,2,0:T(8,128)(2,1)}, u32[]{:S(2)}) copy-start(bf16[16,320,32]{1,2,0:T(8,128)(2,1)} %copy-done.7) | copy-start | bytes 983044
  570.1 251.6 %copy-start.10 = (bf16[16,320,32]{1,2,0:T(8,128)(2,1)S(1)}, bf16[16,320,32]{1,2,0:T(8,128)(2,1)}, u32[]{:S(2)}) copy-start(bf16[16,320,32]{1,2,0:T(8,128)(2,1)} %copy-done.9) | copy-start | bytes 983044
Sparse Core Ops, SparseCore 0:
  830.8 87.6 all-reduce.4
